TPU v7x, 768 devices: a whole 4x8x12 slice. The times are simulated.
768 devices in a mesh: section: 8 (over y), fsdp: 96 (over z, x, core).
Axes of the slice: x: 4, y: 8, z: 12, core: 2. Of those that a mesh axis runs over, the one named last changes fastest.
Arguments:
- master: float32 [8, 768, 4096], P('section', 'fsdp'), may hold values from -0.12 to 0.12
- first_moment: float32 [8, 768, 4096], P('section', 'fsdp'), may hold values from -0.2 to 0.2
- second_moment: float32 [8, 768, 4096], P('section', 'fsdp'), may hold values from 0.25 to 1
- gradient: float32 [8, 768, 4096], P('section', 'fsdp'), may hold values from -64 to 64
Outputs:
- new_master: float32 [8, 768, 4096], P('section', 'fsdp')
- new_first: float32 [8, 768, 4096], P('section', 'fsdp')
- new_second: float32 [8, 768, 4096], P('section', 'fsdp')
- weights: bfloat16 [8, 768, 4096], P('section')
- grad_rms: float32 [], replicated
All inputs are finite; a program needn't handle non-finite values.
Results may differ from a plain program's by a relative error of at most 0.001.
Values may be sent and summed in bfloat16 or wider, within the bound.
No kernel may reach another device: no remote copies, remote signals or barrier semaphores. Data moves between devices by JAX's collectives and lax.ppermute only.
A program may use at most 64 MiB of HBM per device.

v0:
```python
import jax
import jax.numpy as jnp
from jax import lax
from jax.sharding import Mesh
from jax.sharding import PartitionSpec as P

FSDP = ("fsdp_0", "fsdp_1", "fsdp_2")


BETA_ONE = 0.9
BETA_TWO = 0.95
LEARN_RATE = 0.05
DECAY = 0.1
EPSILON = 1e-08
BIAS_STEPS = 10.0


def one_axis_at_a_time(x, axes):
    for axis in axes:
        x = lax.psum(x, axis)
    return x


def copy_for_each(x, axis):
    count = lax.axis_size(axis)
    return lax.all_to_all(jnp.broadcast_to(x[None], (count, *x.shape)), axis, 0, 0, tiled=True)


def taken_together(x, axis):
    everything = copy_for_each(x, axis)
    return jnp.sum(everything, axis=0)


def laid_out(blocks, dim):
    lengths = list(blocks.shape[1:])
    lengths[dim] *= blocks.shape[0]
    return jnp.moveaxis(blocks, 0, dim).reshape(lengths)


def all_blocks(x, axes, order):
    blocks = x[None]
    for k in order:
        blocks = lax.all_gather(blocks, axes[k], axis=0, tiled=True)
    carried = [lax.axis_size(axes[k]) for k in reversed(order)]
    blocks = blocks.reshape(*carried, *x.shape)
    turned = sorted(range(len(order)), key=lambda place: order[len(order) - 1 - place])
    return blocks.transpose(*turned, *range(len(order), blocks.ndim)).reshape(-1, *x.shape)


def gather_axes(x, axes, order, dim):
    return laid_out(all_blocks(x, axes, order), dim)


def adamw_part(master, first_moment, second_moment, gradient, clip_scale):
    scaled = clip_scale * gradient
    new_first = BETA_ONE * first_moment + (1.0 - BETA_ONE) * scaled
    new_second = BETA_TWO * second_moment + (1.0 - BETA_TWO) * scaled * scaled
    first_hat = new_first / (1.0 - BETA_ONE**BIAS_STEPS)
    second_hat = new_second / (1.0 - BETA_TWO**BIAS_STEPS)
    update = first_hat / (jnp.sqrt(second_hat) + EPSILON)
    new_master = master * (1.0 - LEARN_RATE * DECAY) - LEARN_RATE * update
    return (new_master, new_first, new_second)


def local(master, first_moment, second_moment, gradient):
    partial_sq = jnp.sum(gradient * gradient)
    within = one_axis_at_a_time(partial_sq, FSDP)
    squares = taken_together(within, "section")
    grad_norm = jnp.sqrt(squares)
    param_count = float(
        lax.axis_size("section")
        * lax.axis_size(FSDP)
        * gradient.shape[0]
        * gradient.shape[1]
        * gradient.shape[2]
    )
    limit = jnp.float32(0.5 * param_count**0.5)
    clip_scale = limit / jnp.maximum(grad_norm, limit)
    grad_rms = grad_norm / jnp.float32(param_count**0.5)
    new_master, new_first, new_second = adamw_part(
        master, first_moment, second_moment, gradient, clip_scale
    )
    weights = gather_axes(new_master.astype(jnp.bfloat16), FSDP, (1, 0, 2), 1)
    return (new_master, new_first, new_second, weights, grad_rms)


def solution(mesh):
    torus = Mesh(
        mesh.devices.reshape(mesh.shape["section"], 12, 4, 2),
        ("section", "fsdp_0", "fsdp_1", "fsdp_2"),
    )
    placed = (
        P("section", FSDP, None),
        P("section", FSDP, None),
        P("section", FSDP, None),
        P("section", FSDP, None),
    )
    return jax.shard_map(
        local,
        mesh=torus,
        in_specs=placed,
        out_specs=(
            P("section", FSDP, None),
            P("section", FSDP, None),
            P("section", FSDP, None),
            P("section", None, None),
            P(),
        ),
        check_vma=False,
    )
```

profile of v0, /device:TPU:1, one launch (start us, length us, event | category | flops | bytes accessed | tf_op | source)
XLA Modules:
  0.0 184.5 jit_solution(16688505351133183355)
XLA Ops:
  7.2 0.0 all-gather.6.cloned.1.call-start
  7.2 1.5 multiply_reduce_fusion
  8.8 29.2 %psum.21 = f32[]{:T(128)} all-reduce(f32[]{:T(128)} %multiply_reduce_fusion), channel_id=1, replica_groups=mesh['section'=8,'fsdp_0'=12,'fsdp_1'=4,'fsdp_2'=2] {'fsdp_0'}, use_global_device_ids=true, to_apply=%region_1.0 | all-reduce | flops 1 | bytes 8 | tf_op jit(solution)/shard_map/psum | solution.py:20
  38.0 9.2 %psum.22 = f32[]{:T(128)} all-reduce(f32[]{:T(128)} %psum.21), channel_id=1, replica_groups=mesh['section'=8,'fsdp_0'=12,'fsdp_1'=4,'fsdp_2'=2] {'fsdp_1'}, use_global_device_ids=true, to_apply=%region_2.0 | all-reduce | flops 1 | bytes 8 | tf_op jit(solution)/shard_map/psum | solution.py:20
  47.1 10.8 %psum.23 = f32[]{:T(128)} all-reduce(f32[]{:T(128)} %psum.22), channel_id=1, replica_groups=mesh['section'=8,'fsdp_0'=12,'fsdp_1'=4,'fsdp_2'=2] {'fsdp_2'}, use_global_device_ids=true, to_apply=%region_3.0 | all-reduce | flops 1 | bytes 8 | tf_op jit(solution)/shard_map/psum | solution.py:20
  58.0 0.6 broadcast_in_dim.4
  58.6 13.2 %all_to_all.6 = f32[8,1,1]{2,1,0:T(1,128)S(1)} all-to-all(f32[8,1,1]{2,1,0:T(1,128)S(1)} %broadcast_in_dim.4), channel_id=1, replica_groups=mesh['section'=8,'fsdp_0'=12,'fsdp_1'=4,'fsdp_2'=2] {'section'}, dimensions={0} | all-to-all | bytes 64 | tf_op jit(solution)/shard_map/all_to_all | solution.py:26
  71.8 0.6 reduce_sum.19
  73.1 1.9 %fusion.1 = (bf16[1,8,4096]{2,1,0:T(8,128)(2,1)S(1)}, f32[1,8,4096]{2,1,0:T(8,128)}, f32[1,8,4096]{2,1,0:T(8,128)}, f32[1,8,4096]{2,1,0:T(8,128)}) fusion(f32[1,8,4096]{2,1,0:T(8,128)} %param.4, f32[1,8,4096]{2,1,0:T(8,128)} %param.7, f32[]{:T(128)S(6)} %div.21, f32[1,8,4096]{2,1,0:T(8,128)} %param.5, f32[1,8,4096]{2,1,0:T(8,128)} %param.6), kind=kLoop, calls=%fused_computation.5 | loop fusion | flops 524288 | bytes 983044 | tf_op jit(solution)/shard_map/convert_element_type | solution.py:83
  75.0 10.1 %all-gather = bf16[4,8,4096]{2,1,0:T(8,128)(2,1)} all-gather(bf16[1,8,4096]{2,1,0:T(8,128)(2,1)S(1)} %get-tuple-element.5), channel_id=2, replica_groups=mesh['section'=8,'fsdp_0'=12,'fsdp_1'=4,'fsdp_2'=2] {'fsdp_1'}, dimensions={0}, use_global_device_ids=true | all-gather | bytes 327680 | tf_op jit(solution)/shard_map/all_gather | solution.py:43
  85.1 0.0 all-gather.6.cloned.1.call-update
  85.2 0.0 all-gather.8.cloned.1.call-start
  85.2 48.5 %all-gather.6.cloned.1.call-done = bf16[48,8,4096]{2,1,0:T(8,128)(2,1)} async-done(((bf16[4,8,4096]{2,1,0:T(8,128)(2,1)}), bf16[48,8,4096]{2,1,0:T(8,128)(2,1)}) %all-gather.6.cloned.1.call-update) | async-done | bytes 3145744 | tf_op jit(solution)/shard_map/all_gather | solution.py:43
  133.8 0.0 all-gather.8.cloned.1.call-update
  133.8 36.4 %all-gather.8.cloned.1.call-done = bf16[96,8,4096]{2,1,0:T(8,128)(2,1)} async-done(((bf16[48,8,4096]{2,1,0:T(8,128)(2,1)}), bf16[96,8,4096]{2,1,0:T(8,128)(2,1)}) %all-gather.8.cloned.1.call-update) | async-done | bytes 6291472 | tf_op jit(solution)/shard_map/all_gather | solution.py:43
  170.2 6.3 %copy.13 = bf16[12,4,2,1,8,4096]{5,4,2,1,0,3:T(8,128)(2,1)} copy(bf16[12,4,2,1,8,4096]{5,4,1,0,2,3:T(8,128)(2,1)} %bitcast.4) | data formatting | bytes 12582912 | tf_op jit(solution)/shard_map/transpose | solution.py:47
Async XLA Ops:
  7.2 126.6 %all-gather.6.cloned.1.call-start = ((), (), s32[]{:S(2)}) async-start(), calls=%async_computation.1 | async-start | bytes 3407872 | tf_op jit(solution)/shard_map/all_gather | solution.py:43
  85.2 85.1 %all-gather.8.cloned.1.call-start = ((), (), s32[]{:S(2)}) async-start(), calls=%async_computation.2 | async-start | bytes 9437184 | tf_op jit(solution)/shard_map/all_gather | solution.py:43
Sparse Core Ops, SparseCore 0:
  85.3 48.4 all-gather.5
  136.1 34.0 all-gather.7
where the time goes:
time: 185 us; the launch traced here: 184 us
  waiting for transfers between devices  85 us (46%)
  blocking collectives  72.5 us (39%)
  between operations  15.9 us (9%)
  local copies, waits for them, and re-layouts  6.93 us (4%)
  other arithmetic  4.05 us (2%)
    all_gather x2, waiting for transfers between devices, all_blocks(): blocks = lax.all_gather(blocks, axes[k], axis=0, tiled=True)  85 us
    psum x3, blocking collectives, one_axis_at_a_time(): x = lax.psum(x, axis)  49.2 us
    all_to_all x1, blocking collectives, copy_for_each(): lax.all_to_all(jnp.broadcast_to(x[None], (count, *x.shape)), axis, 0, 0,...  13.2 us
    all_gather x1, blocking collectives, all_blocks(): blocks = lax.all_gather(blocks, axes[k], axis=0, tiled=True)  10.1 us
    transpose x1, local copies, waits for them, and re-layouts, all_blocks(): blocks.transpose(*turned, *range(len(order), blocks.ndim))  6.28 us
  transfers between devices with their start and end apart: 2, of which 2 were waited for; matrix products, arithmetic and copies ran while one was open for 0% of the time, Pallas kernels for 0%

commit v1 on v0

--- a/solution.py
+++ b/solution.py
@@ -64,8 +64,7 @@
 
 def local(master, first_moment, second_moment, gradient):
     partial_sq = jnp.sum(gradient * gradient)
-    within = one_axis_at_a_time(partial_sq, FSDP)
-    squares = taken_together(within, "section")
+    squares = lax.psum(partial_sq, ("section", *FSDP))
     grad_norm = jnp.sqrt(squares)
     param_count = float(
         lax.axis_size("section")
@@ -80,7 +79,7 @@
     new_master, new_first, new_second = adamw_part(
         master, first_moment, second_moment, gradient, clip_scale
     )
-    weights = gather_axes(new_master.astype(jnp.bfloat16), FSDP, (1, 0, 2), 1)
+    weights = lax.all_gather(new_master.astype(jnp.bfloat16), FSDP, axis=1, tiled=True)
     return (new_master, new_first, new_second, weights, grad_rms)
 
 

time: 185 us -> 258 us (1.39)
  blocking collectives: 72.5 us -> 120 us
  waiting for transfers between devices: 85 us -> 112 us
    psum x3 -> x1, blocking collectives: 49.2 us -> 120 us  [local(): squares = lax.psum(partial_sq, ('section', *FSDP))]
    all_gather x2 -> x1, waiting for transfers between devices: 85 us -> 112 us  [local(): lax.all_gather(new_master.astype(jnp.bfloat16), FSDP, axis=1, tiled=True)]
    all_to_all x1 -> x0, blocking collectives: 13.2 us -> none  [copy_for_each(): lax.all_to_all(jnp.broadcast_to(x[None], (count, *x.shape)), axis, 0, 0,...]
    all_gather x1 -> x0, blocking collectives: 10.1 us -> none  [all_blocks(): blocks = lax.all_gather(blocks, axes[k], axis=0, tiled=True)]
    transpose x1 -> x0, local copies, waits for them, and re-layouts: 6.28 us -> none  [all_blocks(): blocks.transpose(*turned, *range(len(order), blocks.ndim))]
    unnamed x0 -> x1, local copies, waits for them, and re-layouts: none -> 6.28 us
  transfers between devices with their start and end apart: 2 -> 1, of which waited for: 2 -> 1; matrix products, arithmetic and copies ran while one was open for 0% -> 0% of each run, Pallas kernels for 0% -> 0%
where the time goes in v1:
time: 258 us
  blocking collectives  120 us (47%)
  waiting for transfers between devices  112 us (43%)
  between operations  15.9 us (6%)
  local copies, waits for them, and re-layouts  6.28 us (2%)
  other arithmetic  3.46 us (1%)
    psum x1, blocking collectives, local(): squares = lax.psum(partial_sq, ('section', *FSDP))  120 us
    all_gather x1, waiting for transfers between devices, local(): lax.all_gather(new_master.astype(jnp.bfloat16), FSDP, axis=1, tiled=True)  112 us
    unnamed x1, local copies, waits for them, and re-layouts  6.28 us
  transfers between devices with their start and end apart: 1, of which 1 were waited for; matrix products, arithmetic and copies ran while one was open for 0% of the time, Pallas kernels for 0%

profile of v1, /device:TPU:1, one launch (start us, length us, event | category | flops | bytes accessed | tf_op | source)
XLA Modules:
  0.0 257.7 jit_solution(11529393883070911925)
XLA Ops:
  7.2 0.0 all-gather.2.cloned.1.call-start
  7.2 1.5 multiply_reduce_fusion
  8.8 120.4 %psum.7 = f32[]{:T(128)} all-reduce(f32[]{:T(128)} %multiply_reduce_fusion), channel_id=1, replica_groups=mesh['section'=8,'fsdp_0'=12,'fsdp_1'=4,'fsdp_2'=2] {'section','fsdp_0',..., use_global_device_ids=true, to_apply=%region_1.0 | all-reduce | flops 1 | bytes 8 | tf_op jit(solution)/shard_map/psum | solution.py:67
  129.9 1.9 fusion.1
  131.8 0.0 all-gather.2.cloned.1.call-update
  131.9 111.6 %all-gather.2.cloned.1.call-done = bf16[1,768,4096]{2,1,0:T(8,128)(2,1)} async-done(((bf16[1,8,4096]{2,1,0:T(8,128)(2,1)}), bf16[1,768,4096]{2,1,0:T(8,128)(2,1)}) %all-gather.2.cloned.1.call-update) | async-done | bytes 6291472 | tf_op jit(solution)/shard_map/all_gather | solution.py:82
  243.5 6.3 %copy.10 = bf16[1,768,4096]{2,1,0:T(8,128)(2,1)} copy(bf16[1,768,4096]{2,1,0:T(8,128)(2,1)} %all-gather.2.cloned.1.call-done) | data formatting | bytes 12582912
Async XLA Ops:
  7.2 236.3 %all-gather.2.cloned.1.call-start = ((), (), s32[]{:S(2)}) async-start(), calls=%async_computation | async-start | bytes 6356992 | tf_op jit(solution)/shard_map/all_gather | solution.py:82
Sparse Core Ops, SparseCore 0:
  132.0 111.4 all-gather.1
